TPU v7x, 32 devices: a whole 2x2x4 slice. The times are simulated.
32 devices in a mesh: row: 8 (over z, y), col: 4 (over x, core).
Axes of the slice: x: 2, y: 2, z: 4, core: 2. Of those that a mesh axis runs over, the one named last changes fastest.
Arguments:
- new_dosage: float32 [4096, 1024], P(('col', 'row')), may hold values from 0 to 2
- old_dosage: float32 [16384, 1024], P(('row', 'col')), may hold values from 0 to 2
- grm: bfloat16 [16384, 4096], P('row', 'col'), may hold values from -1.5 to 1.5
- counts: int32 [8], P('col'), may hold values from 256 to 512
- affected: int32 [32, 8], P('row', 'col'), may hold values from 0 to 1, as said below
Outputs:
- updated: bfloat16 [16384, 4096], P('row', 'col')
Inputs may be any that keep to these rules, and one draw needn't show every extreme that they name: `affected`: the density of marked tile pairs differs from one tile of new samples to the next.
All inputs are finite; a program needn't handle non-finite values.
Results may differ from a plain program's by a relative error of at most 0.00115.
Values may be sent and summed in bfloat16 or wider, within the bound.
A program may use at most 128 MiB of HBM per device.

v0:
```python
import functools

import jax
import jax.numpy as jnp
from jax import lax
from jax.experimental import pallas as pl
from jax.experimental.pallas import tpu as pltpu
from jax.sharding import PartitionSpec as P

MESH = pl.DeviceIdType.MESH
CORES = 2
OLD_CHUNKS = 4
NEW_CHUNKS = 2
CODED = 2
PAIR = 2
FOLD = 128
LEVELS = 32767
STRIP = 32


def kernel(
    n_row, n_col, new_hbm, old_hbm, grm_hbm, counts_ref, affected_ref, out_ref,
    new_in, old_in, grm_in, new_code, old_code, new_buf, old_buf, part, part_row,
    load_sem, col_send, col_recv, row_send, row_recv,
    x_send, sib_send, old_recv, right_send, left_send, y_send, new_recv,
):
    snps = new_in.shape[1]
    new_rows, old_rows = new_in.shape[0], old_in.shape[0]
    out_rows, out_cols = out_ref.shape
    tile = out_cols // counts_ref.shape[0]
    minor = 1 << ((n_row.bit_length() - 1) // 2)
    major = n_row // minor
    chips = n_col // CORES
    old_chunk, new_chunk = old_rows // OLD_CHUNKS, new_rows // NEW_CHUNKS
    group = minor * new_rows
    folds = snps // FOLD

    row, col = lax.axis_index("row"), lax.axis_index("col")
    a, b = row // minor, row % minor
    chip, core = col // CORES, col % CORES
    sibling = chip * CORES + (CORES - 1 - core)

    old_load = pltpu.make_async_copy(old_hbm, old_in, load_sem.at[0])
    new_load = pltpu.make_async_copy(new_hbm, new_in, load_sem.at[1])
    grm_load = pltpu.make_async_copy(grm_hbm, grm_in, load_sem.at[2])
    old_load.start()
    new_load.start()

    barrier = pltpu.get_barrier_semaphore()
    for d in range(1, n_col):
        pl.semaphore_signal(barrier, inc=1, device_id=(row, (col + d) % n_col), device_id_type=MESH)
    for d in range(1, n_row):
        pl.semaphore_signal(barrier, inc=1, device_id=((row + d) % n_row, col), device_id_type=MESH)

    old_load.wait()
    grm_load.start()
    mine = jnp.sum(old_in[...], axis=0, keepdims=True)
    for f in range(folds):
        part[pl.ds(col, 1), f, :] = mine[:, f * FOLD:(f + 1) * FOLD]
    def ds(start, size, step):
        return pl.ds(pl.multiple_of(start, step), size)

    def score_place(j, k):
        return ((j // CORES * OLD_CHUNKS + k) * CORES + j % CORES) * old_chunk

    def code_place(j, k):
        return ((j // CORES * CODED + k) * CORES + j % CORES) * old_chunk

    def old_part(j, k):
        if k < CODED:
            return old_code.at[ds(code_place(j, k), old_chunk, old_chunk), :]
        return exact_part(j, k)

    def exact_part(j, k):
        return old_buf.at[ds(score_place(j, k), old_chunk, old_chunk), :]

    def new_part(r, k):
        return new_code.at[ds(r * new_rows + k * new_chunk, new_chunk, new_chunk), :]

    def old_copy(j, k, send, to):
        return pltpu.make_async_remote_copy(
            old_part(j, k), old_part(j, k), send, old_recv.at[j, k],
            device_id=(row, to), device_id_type=MESH,
        )

    def own_copy(j, k):
        return pltpu.make_async_remote_copy(
            exact_part(j, k), exact_part(j, k), sib_send.at[0, k], old_recv.at[j, k],
            device_id=(row, sibling), device_id_type=MESH,
        )

    def new_copy(r, k, send, to):
        return pltpu.make_async_remote_copy(
            new_part(r, k), new_part(r, k), send, new_recv.at[r, k],
            device_id=(to, col), device_id_type=MESH,
        )

    sends = []

    def start(copy, cond=None):
        if cond is None:
            copy.start()
        else:
            @pl.when(cond)
            def _():
                copy.start()
        sends.append((cond, copy))

    def send_y(z, s, k):
        return [
            new_copy(z * minor + b, k, y_send.at[s, d, k], a * minor + (b + d) % minor)
            for d in range(1, minor)
        ]

    def encode(x):
        return ((x * LEVELS + 0.5).astype(jnp.int32) - LEVELS).astype(jnp.int16)

    new_load.wait()
    new_code[ds(row * new_rows, new_rows, new_rows), :] = encode(new_in[...])
    for k in range(CODED):
        old_code[ds(code_place(col, k), old_chunk, old_chunk), :] = encode(
            old_in[k * old_chunk:(k + 1) * old_chunk, :]
        )

    def send_new(k):
        start(new_copy(row, k, right_send.at[0, k], row + minor), a < major - 1)
        start(new_copy(row, k, left_send.at[0, k], row - minor), a > 0)
        for copy in send_y(a, 0, k):
            start(copy)

    def send_old(k):
        for d in range(1, chips):
            start(old_copy(col, k, x_send.at[d, k], (chip + d) % chips * CORES + core))

    def send_sums(buf, me, count, send, recv, target):
        for d in range(1, count):
            pltpu.make_async_remote_copy(
                buf.at[me], buf.at[me], send.at[d], recv.at[me],
                device_id=target((me + d) % count), device_id_type=MESH,
            ).start()

    def take_sums(buf, me, count, send, recv, target):
        for d in range(1, count):
            other = (me + d) % count
            pltpu.make_async_remote_copy(
                buf.at[other], buf.at[other], send.at[d], recv.at[other],
                device_id=target(other), device_id_type=MESH,
            ).wait()
        total = buf[0]
        for i in range(1, count):
            total = total + buf[i]
        return total

    over_col = (part, col, n_col, col_send, col_recv, lambda i: (row, i))
    over_row = (part_row, row, n_row, row_send, row_recv, lambda i: (i, col))

    pl.semaphore_wait(barrier, n_col - 1 + n_row - 1)
    send_sums(*over_col)
    send_new(0)
    for k in range(CODED):
        send_old(k)
    part_row[row] = take_sums(*over_col)
    send_sums(*over_row)
    for k in range(1, NEW_CHUNKS):
        send_new(k)

    def relay(s):
        for k in range(NEW_CHUNKS):
            for left in (True, False):
                z = a - 1 - s if left else a + 1 + s
                valid = z >= 0 if left else z < major
                onward = valid & (a < major - 1) if left else valid & (a > 0)
                r = z * minor + b
                dest = row + minor if left else row - minor
                send = right_send if left else left_send

                @pl.when(valid)
                def _():
                    new_copy(r, k, send.at[s + 1, k], row).wait_recv()
                start(new_copy(r, k, send.at[s + 1, k], dest), onward)
                slot = 1 + 2 * s + (0 if left else 1)
                for copy in send_y(z, slot, k):
                    start(copy, valid)

    def wait_y(z):
        for k in range(NEW_CHUNKS):
            for d in range(1, minor):
                r = z * minor + (b + d) % minor
                new_copy(r, k, y_send.at[0, d, k], row).wait_recv()

    def forward_old(k):
        for d in range(1, chips):
            j = (chip + d) % chips * CORES + core
            old_copy(j, k, sib_send.at[d, k], sibling).wait_recv()
            start(old_copy(j, k, sib_send.at[d, k], sibling))

    def wait_sib_own():
        for k in range(OLD_CHUNKS):
            own_copy(sibling, k).wait_recv()

    def wait_sib_forwarded(k):
        for d in range(1, chips):
            j = (chip + d) % chips * CORES + (CORES - 1 - core)
            old_copy(j, k, sib_send.at[d, k], sibling).wait_recv()

    def block(z, where, k0, count):
        cols = ds(z * group, group, group)
        unit = CORES * old_chunk
        product = lax.dot_general(
            old_buf[ds((where * OLD_CHUNKS + k0) * unit, count * unit, unit), :], new_buf[cols, :],
            (((1,), (1,)), ((), ())), preferred_element_type=jnp.float32,
        )
        for i in range(count):
            for c in range(CORES):
                first = (where * CORES + c) * old_rows + (k0 + i) * old_chunk
                rows = ds(first, old_chunk, old_chunk)
                mark = affected_ref[(z * group) // tile, first // tile].astype(jnp.float32)
                at = (i * CORES + c) * old_chunk
                out_ref[rows, cols] = (
                    grm_in[rows, cols].astype(jnp.float32)
                    + product[at:at + old_chunk, :] * (mark / snps)
                ).astype(jnp.bfloat16)

    def local_rows(z):
        @pl.loop(0, OLD_CHUNKS // PAIR)
        def _(i):
            block(z, chip, i * PAIR, PAIR)

    def far_rows(z, k0, count):
        for d in range(1, chips):
            block(z, (chip + d) % chips, k0, count)

    both = (core, CORES - 1 - core)

    def step_groups(s, body):
        for left in (True, False):
            z = a - 1 - s if left else a + 1 + s

            @pl.when(z >= 0 if left else z < major)
            def _():
                body(z)

    relay(0)
    total = take_sums(*over_row)
    totals = jnp.concatenate([total[f:f + 1] for f in range(folds)], axis=1)
    doubled = totals / (old_rows * n_row * n_col)
    inverse = 1.0 / jnp.sqrt(doubled * (1.0 - 0.5 * doubled) + 0.1)
    code_scale = inverse / LEVELS
    code_shift = (1.0 - doubled) * inverse

    for k in reversed(range(OLD_CHUNKS)):
        rows = old_in[k * old_chunk:(k + 1) * old_chunk, :]
        old_buf[ds(score_place(col, k), old_chunk, old_chunk), :] = (
            (rows - doubled) * inverse
        ).astype(jnp.bfloat16)
    for k in range(CODED, OLD_CHUNKS):
        send_old(k)
    for k in range(OLD_CHUNKS):
        start(own_copy(col, k))
    grm_load.wait()

    def decode(codes):
        return codes.astype(jnp.int32).astype(jnp.float32) * code_scale + code_shift

    def decode_new(z):
        count = counts_ref[(z * group) // tile]

        @pl.loop(0, group // STRIP)
        def _(i):
            at = z * group + i * STRIP
            place = lax.broadcasted_iota(jnp.int32, (STRIP, 1), 0) + at % tile
            usable = (place < count).astype(jnp.float32)
            rows = ds(at, STRIP, STRIP)
            new_buf[rows, :] = (decode(new_code[rows, :]) * usable).astype(jnp.bfloat16)

    def decode_old(k):
        if k >= CODED:
            return
        for d in range(1, chips):
            for c in both:
                j = (chip + d) % chips * CORES + c

                @pl.loop(0, old_chunk // STRIP)
                def _(i):
                    codes = old_code[ds(code_place(j, k) + i * STRIP, STRIP, STRIP), :]
                    old_buf[ds(score_place(j, k) + i * STRIP, STRIP, STRIP), :] = (
                        decode(codes).astype(jnp.bfloat16)
                    )

    forward_old(0)
    wait_y(a)
    decode_new(a)
    wait_sib_own()
    local_rows(a)
    for s in range(1, major - 1):
        relay(s)
        if s < OLD_CHUNKS - 1:
            forward_old(s)
    for k in range(major - 1, OLD_CHUNKS - 1):
        forward_old(k)
    for k in range(OLD_CHUNKS - 1):
        wait_sib_forwarded(k)
        decode_old(k)
    far_rows(a, 0, OLD_CHUNKS - 1)
    last = OLD_CHUNKS - 1

    def most(z):
        wait_y(z)
        decode_new(z)
        local_rows(z)
        far_rows(z, 0, last)

    for s in range(major - 2):
        step_groups(s, most)
    forward_old(last)

    step_groups(major - 2, most)
    wait_sib_forwarded(last)

    @pl.loop(0, major)
    def _(z):
        far_rows(z, last, 1)

    for cond, copy in sends:
        if cond is None:
            copy.wait_send()
        else:
            @pl.when(cond)
            def _():
                copy.wait_send()


def on_device(new_dosage, old_dosage, grm, counts, affected):
    n_row, n_col = lax.axis_size("row"), lax.axis_size("col")
    new_rows, snps = new_dosage.shape
    old_rows = old_dosage.shape[0]
    minor = 1 << ((n_row.bit_length() - 1) // 2)
    major = n_row // minor
    chips = n_col // CORES
    dma = pltpu.SemaphoreType.DMA
    hbm = pl.BlockSpec(memory_space=pltpu.HBM)
    smem = pl.BlockSpec(memory_space=pltpu.SMEM)
    return pl.pallas_call(
        functools.partial(kernel, n_row, n_col),
        out_shape=pltpu.VMEM(grm.shape, grm.dtype),
        in_specs=[hbm, hbm, hbm, smem, smem],
        out_specs=pl.BlockSpec(memory_space=pltpu.VMEM),
        scratch_shapes=[
            pltpu.VMEM((new_rows, snps), jnp.float32),
            pltpu.VMEM((old_rows, snps), jnp.float32),
            pltpu.VMEM(grm.shape, grm.dtype),
            pltpu.VMEM((new_rows * n_row, snps), jnp.int16),
            pltpu.VMEM((old_rows // OLD_CHUNKS * CODED * n_col, snps), jnp.int16),
            pltpu.VMEM((new_rows * n_row, snps), jnp.bfloat16),
            pltpu.VMEM((old_rows * n_col, snps), jnp.bfloat16),
            pltpu.VMEM((n_col, snps // FOLD, FOLD), jnp.float32),
            pltpu.VMEM((n_row, snps // FOLD, FOLD), jnp.float32),
            dma((3,)),
            dma((n_col,)),
            dma((n_col,)),
            dma((n_row,)),
            dma((n_row,)),
            dma((chips, OLD_CHUNKS)),
            dma((chips, OLD_CHUNKS)),
            dma((n_col, OLD_CHUNKS)),
            dma((major, NEW_CHUNKS)),
            dma((major, NEW_CHUNKS)),
            dma((2 * major, minor, NEW_CHUNKS)),
            dma((n_row, NEW_CHUNKS)),
        ],
        compiler_params=pltpu.CompilerParams(
            collective_id=0, has_side_effects=True, vmem_limit_bytes=56 * 1024 * 1024
        ),
    )(new_dosage, old_dosage, grm, counts, affected.T)


def solution(mesh):
    return jax.shard_map(
        on_device,
        mesh=mesh,
        in_specs=(
            P(("col", "row"), None),
            P(("row", "col"), None),
            P("row", "col"),
            P("col"),
            P("row", "col"),
        ),
        out_specs=P("row", "col"),
        check_vma=False,
    )
```

profile of v0, /device:TPU:0, one launch (start us, length us, event | category | flops | bytes accessed | tf_op | source)
XLA Modules:
  0.0 38.2 jit_solution(530347760559102269)
XLA Ops:
  0.0 36.2 %shard_map.55 = bf16[2048,1024]{1,0:T(8,128)(2,1)S(1)} custom-call(f32[128,1024]{1,0:T(8,128)} %new_hbm.1, f32[512,1024]{1,0:T(8,128)} %old_hbm.1, bf16[2048,1024]{1,0:T(8,128)(2,1)} %grm_hbm.1, s32[2]{0:T(128)} %counts_ref.1, s32[2,4]{1,0:T(2,128)} %bitcast.1), custom_call_target="tpu_custom_call" | custom-call | tf_op jit(solution)/shard_map/pallas_call | solution.py:343
  36.2 2.0 %copy.7 = bf16[2048,1024]{1,0:T(8,128)(2,1)} copy(bf16[2048,1024]{1,0:T(8,128)(2,1)S(1)} %shard_map.55) | data formatting | bytes 8388608
where the time goes:
time: 38.7 us; the launch traced here: 38.2 us
  Pallas kernels  36.2 us (94%)
  local copies, waits for them, and re-layouts  2.02 us (5%)
    pallas_call x1, Pallas kernels, on_device(): pl.pallas_call(functools.partial(kernel, n_row, n_col), out_shape=pltpu.V...  36.2 us
    unnamed x1, local copies, waits for them, and re-layouts  2.02 us

commit v1 on v0

v1 whole, which is shorter than its diff:
```python
import functools

import jax
import jax.numpy as jnp
from jax import lax
from jax.experimental import pallas as pl
from jax.experimental.pallas import tpu as pltpu
from jax.sharding import PartitionSpec as P

MESH = pl.DeviceIdType.MESH
CORES = 2
SPLIT = (4, 4, 4, 2, 2)
CODED = 3
NEW_CHUNKS = 2
FOLD = 128
LEVELS = 32767
STRIP = 32


def sizes_of(n_row, n_col, new_rows, old_rows):
    minor = 1 << ((n_row.bit_length() - 1) // 2)
    whole = sum(SPLIT)
    offs = [old_rows * sum(SPLIT[:k]) // whole for k in range(len(SPLIT) + 1)]
    return minor, n_row // minor, n_col // CORES, offs


def ds(start, size, step):
    return pl.ds(pl.multiple_of(start, step), size)


def slot_place(a, major, t):
    near = jnp.minimum(a, major - 1 - a)
    step = (t + 1) // 2
    both = a - step if t % 2 else a + step
    left = a - (t - near)
    right = a + (t - near)
    one = jnp.where(a > major - 1 - a, left, right)
    return jnp.where(t <= 2 * near, both, one) if t else a


def kernel(
    n_row, n_col, new_hbm, old_hbm, grm_hbm, counts_hbm, affected_hbm,
    res, old_buf, new_buf, gain,
    new_in, old_in, new_code, old_code, part, part_y, part_z, counts, affected,
    load_sem, sum_recv, far, x_recv, sib_recv, own_recv, new_recv, sent,
):
    snps = new_in.shape[1]
    new_rows, old_rows = new_in.shape[0], old_in.shape[0]
    out_rows, out_cols = res.shape
    tile = out_cols // counts.shape[0]
    minor, major, chips, offs = sizes_of(n_row, n_col, new_rows, old_rows)
    pieces = len(offs) - 1
    last = pieces - 1
    new_chunk = new_rows // NEW_CHUNKS
    final = NEW_CHUNKS - 1
    group = minor * new_rows
    folds = snps // FOLD
    unit = new_chunk

    row, col = lax.axis_index("row"), lax.axis_index("col")
    a, b = row // minor, row % minor
    chip, core = col // CORES, col % CORES
    sibling = chip * CORES + (CORES - 1 - core)
    has_left, has_right = a > 0, a < major - 1

    def span(k):
        return offs[k + 1] - offs[k]

    grain = min(span(k) for k in range(pieces))

    cut = offs[1]
    old_loads = [
        pltpu.make_async_copy(
            old_hbm.at[pl.ds(lo, hi - lo), :], old_in.at[pl.ds(lo, hi - lo), :], load_sem.at[i]
        )
        for i, (lo, hi) in enumerate(((0, cut), (cut, old_rows)))
    ]
    new_load = pltpu.make_async_copy(new_hbm, new_in, load_sem.at[2])
    grm_load = pltpu.make_async_copy(grm_hbm, res, load_sem.at[3])
    counts_load = pltpu.make_async_copy(counts_hbm, counts, load_sem.at[4])
    affected_load = pltpu.make_async_copy(affected_hbm, affected, load_sem.at[5])
    old_loads[0].start()
    new_load.start()
    for load in old_loads[1:]:
        load.start()
    counts_load.start()
    affected_load.start()

    barrier = pltpu.get_barrier_semaphore()

    def greet(device):
        pl.semaphore_signal(barrier, inc=1, device_id=device, device_id_type=MESH)

    for d in range(1, n_col):
        greet((row, (col + d) % n_col))
    for d in range(1, minor):
        greet((a * minor + (b + d) % minor, col))

    @pl.when(has_left)
    def _():
        greet((row - minor, col))

    @pl.when(has_right)
    def _():
        greet((row + minor, col))

    def score_place(j, k):
        return j // CORES * (CORES * old_rows) + CORES * offs[k] + j % CORES * span(k)

    def code_place(j, k):
        return j // CORES * (CORES * offs[CODED]) + CORES * offs[k] + j % CORES * span(k)

    def exact_part(j, k):
        return old_buf.at[ds(score_place(j, k), span(k), grain), :]

    def old_part(j, k):
        if k < CODED:
            return old_code.at[ds(code_place(j, k), span(k), grain), :]
        return exact_part(j, k)

    own_start = col * old_rows

    def own_part(k):
        if k < CODED:
            return old_part(col, k)
        return old_buf.at[ds(own_start + offs[k], span(k), grain), :]

    def new_part(r, k):
        return new_code.at[ds(r * new_rows + k * new_chunk, new_chunk, new_chunk), :]

    def far_copy(k, d):
        return pltpu.make_async_remote_copy(
            own_part(k), old_part(col, k), sent.at[0], x_recv.at[chips - d - 1, k],
            device_id=(row, (chip + d) % chips * CORES + core), device_id_type=MESH,
        )

    def far_taken(k, d):
        j = (chip + d) % chips * CORES + core
        return pltpu.make_async_remote_copy(
            old_part(j, k), old_part(j, k), sent.at[0], x_recv.at[d - 1, k],
            device_id=(row, j), device_id_type=MESH,
        )

    def pass_copy(k, d, which):
        j = (chip + d) % chips * CORES + which
        return pltpu.make_async_remote_copy(
            old_part(j, k), old_part(j, k), sent.at[0], sib_recv.at[d - 1, k],
            device_id=(row, sibling), device_id_type=MESH,
        )

    def own_copy(j):
        part_of = old_buf.at[ds(j * old_rows, old_rows, grain), :]
        return pltpu.make_async_remote_copy(
            part_of, part_of, sent.at[0], own_recv.at[0],
            device_id=(row, sibling), device_id_type=MESH,
        )

    def new_copy(r, k, to):
        return pltpu.make_async_remote_copy(
            new_part(r, k), new_part(r, k), sent.at[0], new_recv.at[r, k],
            device_id=(to, col), device_id_type=MESH,
        )

    sends = []

    def start(copy, cond=None):
        if cond is None:
            copy.start()
        else:
            @pl.when(cond)
            def _():
                copy.start()
        sends.append((cond, copy))

    def is_end(z):
        return (z == 0) | (z == major - 1)

    def encode(x):
        return ((x * LEVELS + 0.5).astype(jnp.int32) - LEVELS).astype(jnp.int16)

    def encode_old(k):
        old_code[ds(code_place(col, k), span(k), grain), :] = encode(
            old_in[offs[k]:offs[k + 1], :]
        )

    with jax.named_scope("load"):
        old_loads[0].wait()
        encode_old(0)
        new_load.wait()
        new_code[ds(row * new_rows, new_rows, new_rows), :] = encode(new_in[...])
        for load in old_loads[1:]:
            load.wait()
        grm_load.start()
        mine = jnp.sum(old_in[...], axis=0, keepdims=True)
        for f in range(folds):
            part[pl.ds(col, 1), f, :] = mine[:, f * FOLD:(f + 1) * FOLD]

    def send_sums(buf, me, count, recv, target):
        for d in range(1, count):
            copy = pltpu.make_async_remote_copy(
                buf.at[me], buf.at[me], sent.at[0], recv,
                device_id=target((me + d) % count), device_id_type=MESH,
            )
            start(copy)

    def take_sums(buf, me, count, recv, target):
        rest = buf.at[pl.ds(0, count - 1)]
        pltpu.make_async_copy(rest, rest, recv).wait()
        total = buf[0]
        for i in range(1, count):
            total = total + buf[i]
        return total

    over_col = (part, col, n_col, sum_recv.at[0], lambda i: (row, i))
    over_mid = (part_y, b, minor, sum_recv.at[1], lambda i: (a * minor + i, col))
    over_row = (part_z, a, major, sum_recv.at[2], lambda i: (i * minor + b, col))

    def far_tell(h):
        @pl.when(has_right & (a - (h - 1) >= 0))
        def _():
            pl.semaphore_signal(
                far.at[h - 2], inc=1, device_id=(row + minor, col), device_id_type=MESH
            )

        @pl.when(has_left & (a + (h - 1) <= major - 1))
        def _():
            pl.semaphore_signal(
                far.at[h - 2], inc=1, device_id=(row - minor, col), device_id_type=MESH
            )

    def far_hear(h):
        heard = (a - h >= 0).astype(jnp.int32) + (a + h <= major - 1).astype(jnp.int32)

        @pl.when(heard > 0)
        def _():
            pl.semaphore_wait(far.at[h - 2], heard)

    def send_z(k):
        start(new_copy(row, k, row + minor), has_right)
        start(new_copy(row, k, row - minor), has_left)

    def send_y(z, k, cond=None):
        for d in range(1, minor):
            start(new_copy(z * minor + b, k, a * minor + (b + d) % minor), cond)

    def send_old(k):
        for d in range(1, chips):
            start(far_copy(k, d))

    with jax.named_scope("barrier"):
        pl.semaphore_wait(
            barrier,
            n_col - 1 + minor - 1 + has_left.astype(jnp.int32) + has_right.astype(jnp.int32),
        )
    with jax.named_scope("first"):
        send_sums(*over_col)
        send_old(0)
        send_z(0)
        send_y(a, 0)
        far_tell(2)
        for k in range(1, CODED):
            encode_old(k)
            send_old(k)
        for k in range(1, NEW_CHUNKS):
            send_z(k)
    with jax.named_scope("sumcol"):
        part_y[b] = take_sums(*over_col)
        send_sums(*over_mid)
        for k in range(1, NEW_CHUNKS):
            send_y(a, k)
        for h in range(2, major):
            far_hear(h)
            if h + 1 < major:
                far_tell(h + 1)
    with jax.named_scope("sumy"):
        part_z[a] = take_sums(*over_mid)
        send_sums(*over_row)


    def sided(s):
        for left in (True, False):
            z = a - 1 - s if left else a + 1 + s
            valid = z >= 0 if left else z < major
            onward = valid & (has_right if left else has_left)
            dest = row + minor if left else row - minor
            yield z, valid, onward, dest

    def relay(s, k):
        for z, valid, onward, dest in sided(s):
            r = z * minor + b

            @pl.when(valid)
            def _():
                new_copy(r, k, row).wait_recv()
            start(new_copy(r, k, dest), onward)
            across = valid & jnp.logical_not(is_end(z)) if k == final else valid
            send_y(z, k, across)

    def relay_first(s):
        for z, valid, onward, dest in sided(s):
            for d in range(1, minor):
                r = z * minor + (b + d) % minor

                @pl.when(valid & is_end(z))
                def _():
                    new_copy(r, final, row).wait_recv()
                start(new_copy(r, final, dest), onward & is_end(z))

    def own_first():
        for d in range(1, minor):
            r = a * minor + (b + d) % minor
            new_copy(r, final, row).wait_recv()
            start(new_copy(r, final, row + minor), a == 0)
            start(new_copy(r, final, row - minor), a == major - 1)

    def wait_y(t):
        z = slot_place(a, major, t)
        for k in range(NEW_CHUNKS):
            if t == 0 and k == final:
                continue
            for d in range(1, minor):
                r = z * minor + (b + d) % minor
                copy = new_copy(r, k, row)
                if k < final:
                    copy.wait_recv()
                else:
                    @pl.when(jnp.logical_not(is_end(z)))
                    def _():
                        copy.wait_recv()

    def forward_old(k):
        for d in range(1, chips):
            far_taken(k, d).wait_recv()
            start(pass_copy(k, d, core))

    def wait_sib_own():
        own_copy(sibling).wait_recv()

    def wait_sib_forwarded(k):
        for d in range(1, chips):
            pass_copy(k, d, CORES - 1 - core).wait_recv()

    def add(rows, z, product, row_tile):
        cols = ds(z * group, group, group)
        mark = affected[(z * group) // tile, row_tile].astype(jnp.float32)
        res[rows, cols] = (
            res[rows, cols].astype(jnp.float32) + product * (mark / snps)
        ).astype(jnp.bfloat16)

    def product_of(first, height, step, t0, tn):
        return lax.dot_general(
            old_buf[ds(first, height, step), :], new_buf[t0 * group:(t0 + tn) * group, :],
            (((1,), (1,)), ((), ())), preferred_element_type=jnp.float32,
        )

    def block(where, k0, k1, t0, tn):
        low = CORES * offs[k0]
        height = CORES * (offs[k1] - offs[k0])
        product = product_of(where * CORES * old_rows + low, height, grain, t0, tn)
        for i in range(tn):
            z = slot_place(a, major, t0 + i)
            for k in range(k0, k1):
                for c in range(CORES):
                    first = (where * CORES + c) * old_rows + offs[k]
                    at = CORES * offs[k] - low + c * span(k)
                    add(
                        ds(first, span(k), grain), z,
                        product[at:at + span(k), i * group:(i + 1) * group], first // tile,
                    )

    def local_rows(t0, tn):
        step = min(tile, CORES * old_rows)

        @pl.loop(0, CORES * old_rows // step)
        def _(i):
            first = chip * CORES * old_rows + i * step
            product = product_of(first, step, step, t0, tn)
            for j in range(tn):
                add(
                    ds(first, step, step), slot_place(a, major, t0 + j),
                    product[:, j * group:(j + 1) * group], first // tile,
                )

    def far_rows(k0, k1, t0, tn):
        for d in range(1, chips):
            block((chip + d) % chips, k0, k1, t0, tn)

    with jax.named_scope("relay0"):
        relay(0, 0)
    with jax.named_scope("relay1"):
        for k in range(1, NEW_CHUNKS):
            relay(0, k)
    with jax.named_scope("own_first"):
        own_first()
    with jax.named_scope("x0"):
        forward_old(0)
    with jax.named_scope("sumz"):
        total = take_sums(*over_row)
    totals = jnp.concatenate([total[f:f + 1] for f in range(folds)], axis=1)
    doubled = totals / (old_rows * n_row * n_col)
    inverse = 1.0 / jnp.sqrt(doubled * (1.0 - 0.5 * doubled) + 0.1)
    code_scale = inverse / LEVELS
    code_shift = (1.0 - doubled) * inverse

    def score(k):
        old_buf[ds(own_start + offs[k], span(k), grain), :] = (
            (old_in[offs[k]:offs[k + 1], :] - doubled) * inverse
        ).astype(jnp.bfloat16)

    with jax.named_scope("score"):
        for k in range(CODED, pieces):
            score(k)
            send_old(k)
        for k in range(CODED):
            score(k)
        start(own_copy(col))
        counts_load.wait()
        affected_load.wait()
        grm_load.wait()

    def decode(codes):
        return codes.astype(jnp.int32).astype(jnp.float32) * code_scale + code_shift

    def decode_new(t):
        z = slot_place(a, major, t)
        count = counts[(z * group) // tile]

        @pl.loop(0, group // STRIP)
        def _(i):
            at = z * group + i * STRIP
            place = lax.broadcasted_iota(jnp.int32, (STRIP, 1), 0) + at % tile
            usable = (place < count).astype(jnp.float32)
            codes = new_code[ds(at, STRIP, STRIP), :]
            new_buf[ds(t * group + i * STRIP, STRIP, STRIP), :] = (
                decode(codes) * usable
            ).astype(jnp.bfloat16)

    def decode_old(k):
        if k >= CODED:
            return
        strip = min(STRIP, CORES * span(k))
        for d in range(1, chips):
            j = (chip + d) % chips * CORES

            @pl.loop(0, CORES * span(k) // strip)
            def _(i):
                codes = old_code[ds(code_place(j, k) + i * strip, strip, strip), :]
                old_buf[ds(score_place(j, k) + i * strip, strip, strip), :] = (
                    decode(codes).astype(jnp.bfloat16)
                )

    def take_group(t):
        with jax.named_scope("wy%d" % t):
            wait_y(t)
        with jax.named_scope("dec%d" % t):
            decode_new(t)

    def take_old(k):
        with jax.named_scope("ws%d" % k):
            wait_sib_forwarded(k)
            decode_old(k)

    with jax.named_scope("gain"):
        for i in range(out_rows // tile):
            for j in range(out_cols // tile):
                mark = affected[j, i].astype(jnp.float32)
                gain[i:i + 1, j * tile:(j + 1) * tile] = jnp.full(
                    (1, tile), mark / snps, jnp.float32
                )

    def relayed(s, k):
        with jax.named_scope("relay%d_%d" % (s, k)):
            relay(s, k)

    def relayed_first(s):
        with jax.named_scope("first%d" % s):
            relay_first(s)

    def forwarded(k):
        with jax.named_scope("x%d" % k):
            forward_old(k)

    def local(t0, tn):
        with jax.named_scope("mm_local%d" % t0):
            local_rows(t0, tn)

    def distant(k0, k1, t0, tn):
        with jax.named_scope("mm_far%d_%d" % (k0, t0)):
            far_rows(k0, k1, t0, tn)

    half = major // 2
    take_group(0)
    for s in range(1, half):
        relayed(s, 0)
        relayed_first(s - 1)
        relayed(s, 1)
    forwarded(1)
    for t in range(1, half):
        take_group(t)
    with jax.named_scope("sibown"):
        wait_sib_own()
    local(0, half)
    take_old(0)
    take_old(1)
    distant(0, 2, 0, half)
    for s in range(half, major - 1):
        relayed(s, 0)
        relayed_first(s - 1)
        if s == half:
            forwarded(2)
        relayed(s, 1)
    for t in range(half, major - 1):
        take_group(t)
        local(t, 1)
        if t == half:
            take_old(2)
            distant(2, 3, 0, half)
        distant(0, 3, t, 1)
    forwarded(3)
    relayed_first(major - 2)
    take_group(major - 1)
    local(major - 1, 1)
    distant(0, 3, major - 1, 1)
    for k in range(3, pieces):
        take_old(k)
        if k + 1 < pieces:
            distant(k, k + 1, 0, major)
            forwarded(k + 1)

    with jax.named_scope("sends"):
        for cond, copy in sends:
            if cond is None:
                copy.wait_send()
            else:
                @pl.when(cond)
                def _():
                    copy.wait_send()


def finish(n_row, n_col, res, old_buf, new_buf, gain, out_hbm, stage, sem):
    out_rows, out_cols = res.shape
    old_rows, new_rows = out_rows // n_col, out_cols // n_row
    minor, major, chips, offs = sizes_of(n_row, n_col, new_rows, old_rows)
    group = minor * new_rows
    tile = out_rows // gain.shape[0]
    last = len(offs) - 2
    size = offs[last + 1] - offs[last]
    row, col = lax.axis_index("row"), lax.axis_index("col")
    a, chip = row // minor, col // CORES

    def out_copy(src, start, count, i):
        return pltpu.make_async_copy(src, out_hbm.at[ds(start, count, size), :], sem.at[i])

    copies = []
    mine = chip * CORES * old_rows
    copies.append(out_copy(res.at[ds(mine, CORES * old_rows, size), :], mine, CORES * old_rows, 0))
    places = []
    for d in range(1, chips):
        where = (chip + d) % chips
        for c in range(CORES):
            first = (where * CORES + c) * old_rows
            copies.append(out_copy(res.at[ds(first, offs[last], size), :], first, offs[last], len(copies)))
            places.append((d - 1, c, first + offs[last]))
    for copy in copies:
        copy.start()
    with jax.named_scope("tail"):
        for d in range(1, chips):
            where = (chip + d) % chips
            at = where * CORES * old_rows + CORES * offs[last]
            product = lax.dot_general(
                old_buf[ds(at, CORES * size, size), :], new_buf[...],
                (((1,), (1,)), ((), ())), preferred_element_type=jnp.float32,
            )
            for c in range(CORES):
                first = (where * CORES + c) * old_rows + offs[last]
                to = ((d - 1) * CORES + c) * size
                for t in range(major):
                    cols = ds(slot_place(a, major, t) * group, group, group)
                    stage[to:to + size, cols] = (
                        res[ds(first, size, size), cols].astype(jnp.float32)
                        + product[c * size:(c + 1) * size, t * group:(t + 1) * group]
                        * gain[pl.ds(first // tile, 1), cols]
                    ).astype(jnp.bfloat16)
                copy = out_copy(stage.at[pl.ds(to, size), :], first, size, len(copies))
                copy.start()
                copies.append(copy)
    for i, copy in enumerate(copies):
        with jax.named_scope('out%d' % i):
            copy.wait()


def on_device(new_dosage, old_dosage, grm, counts, affected):
    n_row, n_col = lax.axis_size("row"), lax.axis_size("col")
    new_rows, snps = new_dosage.shape
    old_rows = old_dosage.shape[0]
    out_rows, out_cols = grm.shape
    minor, major, chips, offs = sizes_of(n_row, n_col, new_rows, old_rows)
    pieces = len(offs) - 1
    dma = pltpu.SemaphoreType.DMA
    hbm = pl.BlockSpec(memory_space=pltpu.HBM)
    vmem = pl.BlockSpec(memory_space=pltpu.VMEM)
    row_tiles = affected.shape[0]
    res, old_buf, new_buf, gain = pl.pallas_call(
        functools.partial(kernel, n_row, n_col),
        out_shape=(
            pltpu.VMEM(grm.shape, grm.dtype),
            pltpu.VMEM((old_rows * n_col, snps), jnp.bfloat16),
            pltpu.VMEM((new_rows * n_row, snps), jnp.bfloat16),
            pltpu.VMEM((row_tiles, out_cols), jnp.float32),
        ),
        in_specs=[hbm] * 5,
        out_specs=(vmem,) * 4,
        scratch_shapes=[
            pltpu.VMEM((new_rows, snps), jnp.float32),
            pltpu.VMEM((old_rows, snps), jnp.float32),
            pltpu.VMEM((new_rows * n_row, snps), jnp.int16),
            pltpu.VMEM((offs[CODED] * n_col, snps), jnp.int16),
            pltpu.VMEM((n_col, snps // FOLD, FOLD), jnp.float32),
            pltpu.VMEM((minor, snps // FOLD, FOLD), jnp.float32),
            pltpu.VMEM((major, snps // FOLD, FOLD), jnp.float32),
            pltpu.SMEM(counts.shape, jnp.int32),
            pltpu.SMEM(affected.shape[::-1], jnp.int32),
            dma((6,)),
            dma((3,)),
            pltpu.SemaphoreType.REGULAR((max(1, major - 2),)),
            dma((chips - 1, pieces)),
            dma((chips - 1, pieces)),
            dma((1,)),
            dma((n_row, NEW_CHUNKS)),
            dma((1,)),
        ],
        compiler_params=pltpu.CompilerParams(
            collective_id=0, has_side_effects=True, vmem_limit_bytes=50 * 1024 * 1024
        ),
    )(new_dosage, old_dosage, grm, counts, affected.T)
    size = offs[-1] - offs[-2]
    return pl.pallas_call(
        functools.partial(finish, n_row, n_col),
        out_shape=jax.ShapeDtypeStruct(grm.shape, grm.dtype),
        in_specs=[vmem] * 4,
        out_specs=hbm,
        scratch_shapes=[
            pltpu.VMEM(((chips - 1) * CORES * size, out_cols), jnp.bfloat16),
            dma((1 + 2 * (chips - 1) * CORES,)),
        ],
        compiler_params=pltpu.CompilerParams(vmem_limit_bytes=12 * 1024 * 1024),
    )(res, old_buf, new_buf, gain)


def solution(mesh):
    return jax.shard_map(
        on_device,
        mesh=mesh,
        in_specs=(
            P(("col", "row"), None),
            P(("row", "col"), None),
            P("row", "col"),
            P("col"),
            P("row", "col"),
        ),
        out_specs=P("row", "col"),
        check_vma=False,
    )
```

time: 38.7 us -> 33.9 us (0.88)
  Pallas kernels: 36.2 us -> 33.3 us
  local copies, waits for them, and re-layouts: 2.02 us -> 0 us
    pallas_call x1 -> x2, Pallas kernels: 36.2 us -> 33.3 us  [the longest x1 30.7 us: on_device(): pl.pallas_call(functools.partial(kernel, n_row, n_col), out_shape=(pltpu....]
    unnamed x1 -> x0, local copies, waits for them, and re-layouts: 2.02 us -> none
where the time goes in v1:
time: 33.9 us; the launch traced here: 33.4 us
  Pallas kernels  33.3 us (98%)
    pallas_call x1, Pallas kernels, on_device(): pl.pallas_call(functools.partial(kernel, n_row, n_col), out_shape=(pltpu....  30.7 us
    pallas_call x1, Pallas kernels, on_device(): pl.pallas_call(functools.partial(finish, n_row, n_col), out_shape=jax.Sha...  2.69 us

profile of v1, /device:TPU:0, one launch (start us, length us, event | category | flops | bytes accessed | tf_op | source)
XLA Modules:
  0.0 33.4 jit_solution(3062753508303466663)
XLA Ops:
  0.0 30.7 %shard_map.55 = (bf16[2048,1024]{1,0:T(8,128)(2,1)S(1)}, bf16[2048,1024]{1,0:T(8,128)(2,1)S(1)}, bf16[1024,1024]{1,0:T(8,128)(2,1)S(1)}, f32[4,1024]{1,0:T(4,128)S(1)}) custom-call(f32[128,1024]{1,0:T(8,128)} %new_hbm.1, f32[512,1024]{1,0:T(8,128)} %old_hbm.1, bf16[2048,1024]{1,0:T(8,128)(2,1)} %grm_hbm.1, s32[2]{0:T(128)} %counts_hbm.1, s32[2,4]{1,0:T(2,128)} %bitcast.1), custom_call_target="tpu_custom_call" | custom-call | tf_op jit(solution)/shard_map/pallas_call | solution.py:603
  30.7 2.7 %shard_map.56 = bf16[2048,1024]{1,0:T(8,128)(2,1)} custom-call(bf16[2048,1024]{1,0:T(8,128)(2,1)S(1)} %get-tuple-element.9.res, bf16[2048,1024]{1,0:T(8,128)(2,1)S(1)} %get-tuple-element.10.old_buf, bf16[1024,1024]{1,0:T(8,128)(2,1)S(1)} %get-tuple-element.11.new_buf, f32[4,1024]{1,0:T(4,128)S(1)} %get-tuple-element.12.gain), custom_call_target="tpu_custom_call" | custom-call | tf_op jit(solution)/shard_map/pallas_call | solution.py:637

commit v2 on v1

--- a/solution.py
+++ b/solution.py
@@ -11,6 +11,7 @@
 CORES = 2
 SPLIT = (4, 4, 4, 2, 2)
 CODED = 3
+LATE = 3
 NEW_CHUNKS = 2
 FOLD = 128
 LEVELS = 32767
@@ -50,7 +51,6 @@
     tile = out_cols // counts.shape[0]
     minor, major, chips, offs = sizes_of(n_row, n_col, new_rows, old_rows)
     pieces = len(offs) - 1
-    last = pieces - 1
     new_chunk = new_rows // NEW_CHUNKS
     final = NEW_CHUNKS - 1
     group = minor * new_rows
@@ -79,10 +79,9 @@
     grm_load = pltpu.make_async_copy(grm_hbm, res, load_sem.at[3])
     counts_load = pltpu.make_async_copy(counts_hbm, counts, load_sem.at[4])
     affected_load = pltpu.make_async_copy(affected_hbm, affected, load_sem.at[5])
-    old_loads[0].start()
+    for load in old_loads:
+        load.start()
     new_load.start()
-    for load in old_loads[1:]:
-        load.start()
     counts_load.start()
     affected_load.start()
 
@@ -183,18 +182,6 @@
             old_in[offs[k]:offs[k + 1], :]
         )
 
-    with jax.named_scope("load"):
-        old_loads[0].wait()
-        encode_old(0)
-        new_load.wait()
-        new_code[ds(row * new_rows, new_rows, new_rows), :] = encode(new_in[...])
-        for load in old_loads[1:]:
-            load.wait()
-        grm_load.start()
-        mine = jnp.sum(old_in[...], axis=0, keepdims=True)
-        for f in range(folds):
-            part[pl.ds(col, 1), f, :] = mine[:, f * FOLD:(f + 1) * FOLD]
-
     def send_sums(buf, me, count, recv, target):
         for d in range(1, count):
             copy = pltpu.make_async_remote_copy(
@@ -247,17 +234,27 @@
         for d in range(1, chips):
             start(far_copy(k, d))
 
+    with jax.named_scope("loadold"):
+        old_loads[0].wait()
+        encode_old(0)
+        old_loads[1].wait()
+        mine = jnp.sum(old_in[...], axis=0, keepdims=True)
+        for f in range(folds):
+            part[pl.ds(col, 1), f, :] = mine[:, f * FOLD:(f + 1) * FOLD]
     with jax.named_scope("barrier"):
         pl.semaphore_wait(
             barrier,
             n_col - 1 + minor - 1 + has_left.astype(jnp.int32) + has_right.astype(jnp.int32),
         )
+    send_sums(*over_col)
+    send_old(0)
+    far_tell(2)
     with jax.named_scope("first"):
-        send_sums(*over_col)
-        send_old(0)
+        new_load.wait()
+        new_code[ds(row * new_rows, new_rows, new_rows), :] = encode(new_in[...])
         send_z(0)
         send_y(a, 0)
-        far_tell(2)
+        grm_load.start()
         for k in range(1, CODED):
             encode_old(k)
             send_old(k)
@@ -268,6 +265,7 @@
         send_sums(*over_mid)
         for k in range(1, NEW_CHUNKS):
             send_y(a, k)
+    with jax.named_scope("hear"):
         for h in range(2, major):
             far_hear(h)
             if h + 1 < major:
@@ -500,8 +498,8 @@
     with jax.named_scope("sibown"):
         wait_sib_own()
     local(0, half)
-    take_old(0)
-    take_old(1)
+    for k in range(2):
+        take_old(k)
     distant(0, 2, 0, half)
     for s in range(half, major - 1):
         relayed(s, 0)
@@ -512,20 +510,18 @@
     for t in range(half, major - 1):
         take_group(t)
         local(t, 1)
-        if t == half:
-            take_old(2)
-            distant(2, 3, 0, half)
-        distant(0, 3, t, 1)
+        distant(0, 2, t, 1)
+    take_old(2)
+    distant(2, LATE, 0, major - 1)
     forwarded(3)
     relayed_first(major - 2)
     take_group(major - 1)
     local(major - 1, 1)
-    distant(0, 3, major - 1, 1)
-    for k in range(3, pieces):
+    distant(0, LATE, major - 1, 1)
+    for k in range(4, pieces):
+        forwarded(k)
+    for k in range(LATE, pieces):
         take_old(k)
-        if k + 1 < pieces:
-            distant(k, k + 1, 0, major)
-            forwarded(k + 1)
 
     with jax.named_scope("sends"):
         for cond, copy in sends:
@@ -543,49 +539,54 @@
     minor, major, chips, offs = sizes_of(n_row, n_col, new_rows, old_rows)
     group = minor * new_rows
     tile = out_rows // gain.shape[0]
-    last = len(offs) - 2
-    size = offs[last + 1] - offs[last]
+    early, size = offs[LATE], old_rows - offs[LATE]
+    grain = min(hi - lo for lo, hi in zip(offs[:-1], offs[1:], strict=True))
     row, col = lax.axis_index("row"), lax.axis_index("col")
     a, chip = row // minor, col // CORES
 
-    def out_copy(src, start, count, i):
-        return pltpu.make_async_copy(src, out_hbm.at[ds(start, count, size), :], sem.at[i])
-
-    copies = []
+    def out_copy(src, start, count):
+        return pltpu.make_async_copy(
+            src, out_hbm.at[ds(start, count, grain), :], sem.at[0]
+        )
+
     mine = chip * CORES * old_rows
-    copies.append(out_copy(res.at[ds(mine, CORES * old_rows, size), :], mine, CORES * old_rows, 0))
-    places = []
+    copies = [
+        out_copy(res.at[ds(mine, CORES * old_rows, grain), :], mine, CORES * old_rows)
+    ]
     for d in range(1, chips):
-        where = (chip + d) % chips
         for c in range(CORES):
-            first = (where * CORES + c) * old_rows
-            copies.append(out_copy(res.at[ds(first, offs[last], size), :], first, offs[last], len(copies)))
-            places.append((d - 1, c, first + offs[last]))
+            first = ((chip + d) % chips * CORES + c) * old_rows
+            copies.append(out_copy(res.at[ds(first, early, grain), :], first, early))
     for copy in copies:
         copy.start()
     with jax.named_scope("tail"):
         for d in range(1, chips):
             where = (chip + d) % chips
-            at = where * CORES * old_rows + CORES * offs[last]
+            low = where * CORES * old_rows + CORES * early
             product = lax.dot_general(
-                old_buf[ds(at, CORES * size, size), :], new_buf[...],
+                old_buf[ds(low, CORES * size, grain), :], new_buf[...],
                 (((1,), (1,)), ((), ())), preferred_element_type=jnp.float32,
             )
             for c in range(CORES):
-                first = (where * CORES + c) * old_rows + offs[last]
+                start_row = (where * CORES + c) * old_rows + early
                 to = ((d - 1) * CORES + c) * size
-                for t in range(major):
-                    cols = ds(slot_place(a, major, t) * group, group, group)
-                    stage[to:to + size, cols] = (
-                        res[ds(first, size, size), cols].astype(jnp.float32)
-                        + product[c * size:(c + 1) * size, t * group:(t + 1) * group]
-                        * gain[pl.ds(first // tile, 1), cols]
-                    ).astype(jnp.bfloat16)
-                copy = out_copy(stage.at[pl.ds(to, size), :], first, size, len(copies))
+                for k in range(LATE, len(offs) - 1):
+                    span = offs[k + 1] - offs[k]
+                    at = CORES * (offs[k] - early) + c * span
+                    lead = offs[k] - early
+                    first = start_row + lead
+                    for t in range(major):
+                        cols = ds(slot_place(a, major, t) * group, group, group)
+                        stage[to + lead:to + lead + span, cols] = (
+                            res[ds(first, span, grain), cols].astype(jnp.float32)
+                            + product[at:at + span, t * group:(t + 1) * group]
+                            * gain[pl.ds(first // tile, 1), cols]
+                        ).astype(jnp.bfloat16)
+                copy = out_copy(stage.at[pl.ds(to, size), :], start_row, size)
                 copy.start()
                 copies.append(copy)
-    for i, copy in enumerate(copies):
-        with jax.named_scope('out%d' % i):
+    with jax.named_scope("out"):
+        for copy in copies:
             copy.wait()
 
 
@@ -633,7 +634,7 @@
             collective_id=0, has_side_effects=True, vmem_limit_bytes=50 * 1024 * 1024
         ),
     )(new_dosage, old_dosage, grm, counts, affected.T)
-    size = offs[-1] - offs[-2]
+    size = old_rows - offs[LATE]
     return pl.pallas_call(
         functools.partial(finish, n_row, n_col),
         out_shape=jax.ShapeDtypeStruct(grm.shape, grm.dtype),
@@ -641,7 +642,7 @@
         out_specs=hbm,
         scratch_shapes=[
             pltpu.VMEM(((chips - 1) * CORES * size, out_cols), jnp.bfloat16),
-            dma((1 + 2 * (chips - 1) * CORES,)),
+            dma((1,)),
         ],
         compiler_params=pltpu.CompilerParams(vmem_limit_bytes=12 * 1024 * 1024),
     )(res, old_buf, new_buf, gain)

time: 33.9 us -> 32.3 us (0.953)
  Pallas kernels: 33.3 us -> 32 us
    pallas_call x1, Pallas kernels: 30.7 us -> 29.5 us  [on_device(): pl.pallas_call(functools.partial(kernel, n_row, n_col), out_shape=(pltpu....]
where the time goes in v2:
time: 32.3 us; the launch traced here: 32 us
  Pallas kernels  32 us (99%)
    pallas_call x1, Pallas kernels, on_device(): pl.pallas_call(functools.partial(kernel, n_row, n_col), out_shape=(pltpu....  29.5 us
    pallas_call x1, Pallas kernels, on_device(): pl.pallas_call(functools.partial(finish, n_row, n_col), out_shape=jax.Sha...  2.57 us

profile of v2, /device:TPU:0, one launch (start us, length us, event | category | flops | bytes accessed | tf_op | source)
XLA Modules:
  0.0 32.0 jit_solution(3921493870626518952)
XLA Ops:
  0.0 29.5 %shard_map.55 = (bf16[2048,1024]{1,0:T(8,128)(2,1)S(1)}, bf16[2048,1024]{1,0:T(8,128)(2,1)S(1)}, bf16[1024,1024]{1,0:T(8,128)(2,1)S(1)}, f32[4,1024]{1,0:T(4,128)S(1)}) custom-call(f32[128,1024]{1,0:T(8,128)} %new_hbm.1, f32[512,1024]{1,0:T(8,128)} %old_hbm.1, bf16[2048,1024]{1,0:T(8,128)(2,1)} %grm_hbm.1, s32[2]{0:T(128)} %counts_hbm.1, s32[2,4]{1,0:T(2,128)} %bitcast.1), custom_call_target="tpu_custom_call" | custom-call | tf_op jit(solution)/shard_map/pallas_call | solution.py:604
  29.5 2.6 %shard_map.56 = bf16[2048,1024]{1,0:T(8,128)(2,1)} custom-call(bf16[2048,1024]{1,0:T(8,128)(2,1)S(1)} %get-tuple-element.9.res, bf16[2048,1024]{1,0:T(8,128)(2,1)S(1)} %get-tuple-element.10.old_buf, bf16[1024,1024]{1,0:T(8,128)(2,1)S(1)} %get-tuple-element.11.new_buf, f32[4,1024]{1,0:T(4,128)S(1)} %get-tuple-element.12.gain), custom_call_target="tpu_custom_call" | custom-call | tf_op jit(solution)/shard_map/pallas_call | solution.py:638

commit v3 on v2

--- a/solution.py
+++ b/solution.py
@@ -32,7 +32,8 @@
 def slot_place(a, major, t):
     near = jnp.minimum(a, major - 1 - a)
     step = (t + 1) // 2
-    both = a - step if t % 2 else a + step
+    toward = jnp.where(a > major - 1 - a, step, -step)
+    both = a + toward if t % 2 else a - toward
     left = a - (t - near)
     right = a + (t - near)
     one = jnp.where(a > major - 1 - a, left, right)
@@ -68,19 +69,12 @@
 
     grain = min(span(k) for k in range(pieces))
 
-    cut = offs[1]
-    old_loads = [
-        pltpu.make_async_copy(
-            old_hbm.at[pl.ds(lo, hi - lo), :], old_in.at[pl.ds(lo, hi - lo), :], load_sem.at[i]
-        )
-        for i, (lo, hi) in enumerate(((0, cut), (cut, old_rows)))
-    ]
-    new_load = pltpu.make_async_copy(new_hbm, new_in, load_sem.at[2])
-    grm_load = pltpu.make_async_copy(grm_hbm, res, load_sem.at[3])
-    counts_load = pltpu.make_async_copy(counts_hbm, counts, load_sem.at[4])
-    affected_load = pltpu.make_async_copy(affected_hbm, affected, load_sem.at[5])
-    for load in old_loads:
-        load.start()
+    old_load = pltpu.make_async_copy(old_hbm, old_in, load_sem.at[0])
+    new_load = pltpu.make_async_copy(new_hbm, new_in, load_sem.at[1])
+    grm_load = pltpu.make_async_copy(grm_hbm, res, load_sem.at[2])
+    counts_load = pltpu.make_async_copy(counts_hbm, counts, load_sem.at[3])
+    affected_load = pltpu.make_async_copy(affected_hbm, affected, load_sem.at[4])
+    old_load.start()
     new_load.start()
     counts_load.start()
     affected_load.start()
@@ -235,9 +229,7 @@
             start(far_copy(k, d))
 
     with jax.named_scope("loadold"):
-        old_loads[0].wait()
-        encode_old(0)
-        old_loads[1].wait()
+        old_load.wait()
         mine = jnp.sum(old_in[...], axis=0, keepdims=True)
         for f in range(folds):
             part[pl.ds(col, 1), f, :] = mine[:, f * FOLD:(f + 1) * FOLD]
@@ -247,6 +239,7 @@
             n_col - 1 + minor - 1 + has_left.astype(jnp.int32) + has_right.astype(jnp.int32),
         )
     send_sums(*over_col)
+    encode_old(0)
     send_old(0)
     far_tell(2)
     with jax.named_scope("first"):
@@ -486,28 +479,28 @@
         with jax.named_scope("mm_far%d_%d" % (k0, t0)):
             far_rows(k0, k1, t0, tn)
 
-    half = major // 2
     take_group(0)
-    for s in range(1, half):
+    take_old(0)
+    relayed(1, 0)
+    relayed_first(0)
+    with jax.named_scope("sibown"):
+        wait_sib_own()
+    local(0, 1)
+    relayed(1, 1)
+    forwarded(1)
+    distant(0, 1, 0, 1)
+    take_group(1)
+    local(1, 1)
+    distant(0, 1, 1, 1)
+    for s in range(2, major - 1):
         relayed(s, 0)
         relayed_first(s - 1)
-        relayed(s, 1)
-    forwarded(1)
-    for t in range(1, half):
-        take_group(t)
-    with jax.named_scope("sibown"):
-        wait_sib_own()
-    local(0, half)
-    for k in range(2):
-        take_old(k)
-    distant(0, 2, 0, half)
-    for s in range(half, major - 1):
-        relayed(s, 0)
-        relayed_first(s - 1)
-        if s == half:
+        if s == 2:
+            take_old(1)
+            distant(1, 2, 0, 2)
             forwarded(2)
         relayed(s, 1)
-    for t in range(half, major - 1):
+    for t in range(2, major - 1):
         take_group(t)
         local(t, 1)
         distant(0, 2, t, 1)
@@ -517,9 +510,9 @@
     relayed_first(major - 2)
     take_group(major - 1)
     local(major - 1, 1)
-    distant(0, LATE, major - 1, 1)
     for k in range(4, pieces):
         forwarded(k)
+    distant(0, LATE, major - 1, 1)
     for k in range(LATE, pieces):
         take_old(k)
 
@@ -621,7 +614,7 @@
             pltpu.VMEM((major, snps // FOLD, FOLD), jnp.float32),
             pltpu.SMEM(counts.shape, jnp.int32),
             pltpu.SMEM(affected.shape[::-1], jnp.int32),
-            dma((6,)),
+            dma((5,)),
             dma((3,)),
             pltpu.SemaphoreType.REGULAR((max(1, major - 2),)),
             dma((chips - 1, pieces)),

time: 32.3 us -> 32.1 us (level)
  no operation moved by 1% of the time
where the time goes in v3:
time: 32.1 us; the launch traced here: 31.9 us
  Pallas kernels  31.9 us (99%)
    pallas_call x1, Pallas kernels, on_device(): pl.pallas_call(functools.partial(kernel, n_row, n_col), out_shape=(pltpu....  29.4 us
    pallas_call x1, Pallas kernels, on_device(): pl.pallas_call(functools.partial(finish, n_row, n_col), out_shape=jax.Sha...  2.57 us

profile of v3, /device:TPU:0, one launch (start us, length us, event | category | flops | bytes accessed | tf_op | source)
XLA Modules:
  0.0 31.9 jit_solution(9099964548294757635)
XLA Ops:
  0.0 29.4 %shard_map.55 = (bf16[2048,1024]{1,0:T(8,128)(2,1)S(1)}, bf16[2048,1024]{1,0:T(8,128)(2,1)S(1)}, bf16[1024,1024]{1,0:T(8,128)(2,1)S(1)}, f32[4,1024]{1,0:T(4,128)S(1)}) custom-call(f32[128,1024]{1,0:T(8,128)} %new_hbm.1, f32[512,1024]{1,0:T(8,128)} %old_hbm.1, bf16[2048,1024]{1,0:T(8,128)(2,1)} %grm_hbm.1, s32[2]{0:T(128)} %counts_hbm.1, s32[2,4]{1,0:T(2,128)} %bitcast.1), custom_call_target="tpu_custom_call" | custom-call | tf_op jit(solution)/shard_map/pallas_call | solution.py:597
  29.4 2.6 %shard_map.56 = bf16[2048,1024]{1,0:T(8,128)(2,1)} custom-call(bf16[2048,1024]{1,0:T(8,128)(2,1)S(1)} %get-tuple-element.9.res, bf16[2048,1024]{1,0:T(8,128)(2,1)S(1)} %get-tuple-element.10.old_buf, bf16[1024,1024]{1,0:T(8,128)(2,1)S(1)} %get-tuple-element.11.new_buf, f32[4,1024]{1,0:T(4,128)S(1)} %get-tuple-element.12.gain), custom_call_target="tpu_custom_call" | custom-call | tf_op jit(solution)/shard_map/pallas_call | solution.py:631

commit v4 on v3

--- a/solution.py
+++ b/solution.py
@@ -9,7 +9,8 @@
 
 MESH = pl.DeviceIdType.MESH
 CORES = 2
-SPLIT = (4, 4, 4, 2, 2)
+SPLIT = (4, 2, 4, 4, 2)
+AHEAD = 2
 CODED = 3
 LATE = 3
 NEW_CHUNKS = 2
@@ -52,6 +53,7 @@
     tile = out_cols // counts.shape[0]
     minor, major, chips, offs = sizes_of(n_row, n_col, new_rows, old_rows)
     pieces = len(offs) - 1
+    last = pieces - 1
     new_chunk = new_rows // NEW_CHUNKS
     final = NEW_CHUNKS - 1
     group = minor * new_rows
@@ -69,13 +71,19 @@
 
     grain = min(span(k) for k in range(pieces))
 
-    old_load = pltpu.make_async_copy(old_hbm, old_in, load_sem.at[0])
-    new_load = pltpu.make_async_copy(new_hbm, new_in, load_sem.at[1])
-    grm_load = pltpu.make_async_copy(grm_hbm, res, load_sem.at[2])
-    counts_load = pltpu.make_async_copy(counts_hbm, counts, load_sem.at[3])
-    affected_load = pltpu.make_async_copy(affected_hbm, affected, load_sem.at[4])
-    old_load.start()
+    old_loads = [
+        pltpu.make_async_copy(
+            old_hbm.at[pl.ds(lo, hi - lo), :], old_in.at[pl.ds(lo, hi - lo), :], load_sem.at[i]
+        )
+        for i, (lo, hi) in enumerate(((0, offs[1]), (offs[1], old_rows)))
+    ]
+    new_load = pltpu.make_async_copy(new_hbm, new_in, load_sem.at[2])
+    grm_load = pltpu.make_async_copy(grm_hbm, res, load_sem.at[3])
+    counts_load = pltpu.make_async_copy(counts_hbm, counts, load_sem.at[4])
+    affected_load = pltpu.make_async_copy(affected_hbm, affected, load_sem.at[5])
+    old_loads[0].start()
     new_load.start()
+    old_loads[1].start()
     counts_load.start()
     affected_load.start()
 
@@ -224,40 +232,63 @@
         for d in range(1, minor):
             start(new_copy(z * minor + b, k, a * minor + (b + d) % minor), cond)
 
+    lender = core == CORES - 1
+    taker = core != CORES - 1
+
     def send_old(k):
         for d in range(1, chips):
-            start(far_copy(k, d))
-
-    with jax.named_scope("loadold"):
-        old_load.wait()
-        mine = jnp.sum(old_in[...], axis=0, keepdims=True)
-        for f in range(folds):
-            part[pl.ds(col, 1), f, :] = mine[:, f * FOLD:(f + 1) * FOLD]
+            start(far_copy(k, d), lender if k == last else None)
+
+    def lend(d, which):
+        j = (chip + d) % chips * CORES + which
+        return pltpu.make_async_remote_copy(
+            exact_part(j, last), exact_part(j, last), sent.at[0], x_recv.at[d - 1, pieces],
+            device_id=(row, j), device_id_type=MESH,
+        )
+
+    def send_lent():
+        for d in range(1, chips):
+            copy = pltpu.make_async_remote_copy(
+                old_buf.at[ds(sibling * old_rows + offs[last], span(last), grain), :],
+                exact_part(sibling, last), sent.at[0], x_recv.at[chips - d - 1, pieces],
+                device_id=(row, (chip + d) % chips * CORES + core), device_id_type=MESH,
+            )
+            start(copy, lender)
+
+    def pass_lent(d, which):
+        j = (chip + d) % chips * CORES + which
+        return pltpu.make_async_remote_copy(
+            exact_part(j, last), exact_part(j, last), sent.at[0], sib_recv.at[d - 1, pieces],
+            device_id=(row, sibling), device_id_type=MESH,
+        )
+
+    with jax.named_scope("load0"):
+        old_loads[0].wait()
+        encode_old(0)
+        new_load.wait()
+        new_code[ds(row * new_rows, new_rows, new_rows), :] = encode(new_in[...])
     with jax.named_scope("barrier"):
         pl.semaphore_wait(
             barrier,
             n_col - 1 + minor - 1 + has_left.astype(jnp.int32) + has_right.astype(jnp.int32),
         )
-    send_sums(*over_col)
-    encode_old(0)
     send_old(0)
+    send_z(0)
     far_tell(2)
+    with jax.named_scope("loadold"):
+        old_loads[1].wait()
+        mine = jnp.sum(old_in[...], axis=0, keepdims=True)
+        for f in range(folds):
+            part_y[pl.ds(b, 1), f, :] = mine[:, f * FOLD:(f + 1) * FOLD]
+        send_sums(*over_mid)
     with jax.named_scope("first"):
-        new_load.wait()
-        new_code[ds(row * new_rows, new_rows, new_rows), :] = encode(new_in[...])
-        send_z(0)
-        send_y(a, 0)
-        grm_load.start()
+        for k in range(NEW_CHUNKS):
+            send_y(a, k)
         for k in range(1, CODED):
             encode_old(k)
+        for k in range(1, AHEAD):
             send_old(k)
-        for k in range(1, NEW_CHUNKS):
-            send_z(k)
-    with jax.named_scope("sumcol"):
-        part_y[b] = take_sums(*over_col)
-        send_sums(*over_mid)
-        for k in range(1, NEW_CHUNKS):
-            send_y(a, k)
+        grm_load.start()
     with jax.named_scope("hear"):
         for h in range(2, major):
             far_hear(h)
@@ -266,7 +297,8 @@
     with jax.named_scope("sumy"):
         part_z[a] = take_sums(*over_mid)
         send_sums(*over_row)
-
+        for k in range(1, NEW_CHUNKS):
+            send_z(k)
 
     def sided(s):
         for left in (True, False):
@@ -321,15 +353,32 @@
 
     def forward_old(k):
         for d in range(1, chips):
-            far_taken(k, d).wait_recv()
-            start(pass_copy(k, d, core))
+            if k < last:
+                far_taken(k, d).wait_recv()
+                start(pass_copy(k, d, core))
+            else:
+                @pl.when(lender)
+                def _():
+                    far_taken(k, d).wait_recv()
+                start(pass_copy(k, d, core), lender)
+
+                @pl.when(lender)
+                def _():
+                    lend(d, CORES - 1 - core).wait_recv()
+                start(pass_lent(d, CORES - 1 - core), lender)
 
     def wait_sib_own():
         own_copy(sibling).wait_recv()
 
     def wait_sib_forwarded(k):
         for d in range(1, chips):
-            pass_copy(k, d, CORES - 1 - core).wait_recv()
+            if k < last:
+                pass_copy(k, d, CORES - 1 - core).wait_recv()
+            else:
+                @pl.when(taker)
+                def _():
+                    pass_copy(k, d, CORES - 1 - core).wait_recv()
+                    pass_lent(d, core).wait_recv()
 
     def add(rows, z, product, row_tile):
         cols = ds(z * group, group, group)
@@ -378,6 +427,11 @@
 
     with jax.named_scope("relay0"):
         relay(0, 0)
+    with jax.named_scope("sumz"):
+        part[col] = take_sums(*over_row)
+        send_sums(*over_col)
+        for k in range(AHEAD, CODED):
+            send_old(k)
     with jax.named_scope("relay1"):
         for k in range(1, NEW_CHUNKS):
             relay(0, k)
@@ -385,8 +439,8 @@
         own_first()
     with jax.named_scope("x0"):
         forward_old(0)
-    with jax.named_scope("sumz"):
-        total = take_sums(*over_row)
+    with jax.named_scope("sumcol"):
+        total = take_sums(*over_col)
     totals = jnp.concatenate([total[f:f + 1] for f in range(folds)], axis=1)
     doubled = totals / (old_rows * n_row * n_col)
     inverse = 1.0 / jnp.sqrt(doubled * (1.0 - 0.5 * doubled) + 0.1)
@@ -479,39 +533,38 @@
         with jax.named_scope("mm_far%d_%d" % (k0, t0)):
             far_rows(k0, k1, t0, tn)
 
+    forwarded(1)
     take_group(0)
     take_old(0)
     relayed(1, 0)
     relayed_first(0)
     with jax.named_scope("sibown"):
         wait_sib_own()
+        send_lent()
     local(0, 1)
+    take_old(1)
     relayed(1, 1)
-    forwarded(1)
-    distant(0, 1, 0, 1)
+    distant(0, 2, 0, 1)
     take_group(1)
     local(1, 1)
-    distant(0, 1, 1, 1)
+    distant(0, 2, 1, 1)
     for s in range(2, major - 1):
         relayed(s, 0)
         relayed_first(s - 1)
         if s == 2:
-            take_old(1)
-            distant(1, 2, 0, 2)
             forwarded(2)
+            take_old(2)
+            distant(2, 3, 0, 2)
         relayed(s, 1)
     for t in range(2, major - 1):
         take_group(t)
         local(t, 1)
-        distant(0, 2, t, 1)
-    take_old(2)
-    distant(2, LATE, 0, major - 1)
+        distant(0, LATE, t, 1)
     forwarded(3)
     relayed_first(major - 2)
     take_group(major - 1)
     local(major - 1, 1)
-    for k in range(4, pieces):
-        forwarded(k)
+    forwarded(4)
     distant(0, LATE, major - 1, 1)
     for k in range(LATE, pieces):
         take_old(k)
@@ -552,7 +605,15 @@
             copies.append(out_copy(res.at[ds(first, early, grain), :], first, early))
     for copy in copies:
         copy.start()
-    with jax.named_scope("tail"):
+    tails = []
+    for d in range(1, chips):
+        for c in range(CORES):
+            to = ((d - 1) * CORES + c) * size
+            start_row = ((chip + d) % chips * CORES + c) * old_rows + early
+            tails.append(out_copy(stage.at[pl.ds(to, size), :], start_row, size))
+
+    @pl.when(row >= 0)
+    def _():
         for d in range(1, chips):
             where = (chip + d) % chips
             low = where * CORES * old_rows + CORES * early
@@ -561,13 +622,12 @@
                 (((1,), (1,)), ((), ())), preferred_element_type=jnp.float32,
             )
             for c in range(CORES):
-                start_row = (where * CORES + c) * old_rows + early
                 to = ((d - 1) * CORES + c) * size
                 for k in range(LATE, len(offs) - 1):
                     span = offs[k + 1] - offs[k]
-                    at = CORES * (offs[k] - early) + c * span
                     lead = offs[k] - early
-                    first = start_row + lead
+                    at = CORES * lead + c * span
+                    first = (where * CORES + c) * old_rows + offs[k]
                     for t in range(major):
                         cols = ds(slot_place(a, major, t) * group, group, group)
                         stage[to + lead:to + lead + span, cols] = (
@@ -575,11 +635,10 @@
                             + product[at:at + span, t * group:(t + 1) * group]
                             * gain[pl.ds(first // tile, 1), cols]
                         ).astype(jnp.bfloat16)
-                copy = out_copy(stage.at[pl.ds(to, size), :], start_row, size)
-                copy.start()
-                copies.append(copy)
+                tails[(d - 1) * CORES + c].start()
+
     with jax.named_scope("out"):
-        for copy in copies:
+        for copy in copies + tails:
             copy.wait()
 
 
@@ -614,11 +673,11 @@
             pltpu.VMEM((major, snps // FOLD, FOLD), jnp.float32),
             pltpu.SMEM(counts.shape, jnp.int32),
             pltpu.SMEM(affected.shape[::-1], jnp.int32),
-            dma((5,)),
+            dma((6,)),
             dma((3,)),
             pltpu.SemaphoreType.REGULAR((max(1, major - 2),)),
-            dma((chips - 1, pieces)),
-            dma((chips - 1, pieces)),
+            dma((chips - 1, pieces + 1)),
+            dma((chips - 1, pieces + 1)),
             dma((1,)),
             dma((n_row, NEW_CHUNKS)),
             dma((1,)),

time: 32.1 us -> 31.1 us (0.969)
  Pallas kernels: 31.9 us -> 31 us
    pallas_call x1, Pallas kernels: 2.57 us -> 2.03 us  [on_device(): pl.pallas_call(functools.partial(finish, n_row, n_col), out_shape=jax.Sha...]
    pallas_call x1, Pallas kernels: 29.4 us -> 28.9 us  [on_device(): pl.pallas_call(functools.partial(kernel, n_row, n_col), out_shape=(pltpu....]
where the time goes in v4:
time: 31.1 us; the launch traced here: 31 us
  Pallas kernels  31 us (100%)
    pallas_call x1, Pallas kernels, on_device(): pl.pallas_call(functools.partial(kernel, n_row, n_col), out_shape=(pltpu....  28.9 us
    pallas_call x1, Pallas kernels, on_device(): pl.pallas_call(functools.partial(finish, n_row, n_col), out_shape=jax.Sha...  2.03 us

profile of v4, /device:TPU:0, one launch (start us, length us, event | category | flops | bytes accessed | tf_op | source)
XLA Modules:
  0.0 31.0 jit_solution(966402150022854510)
XLA Ops:
  0.0 28.9 %shard_map.55 = (bf16[2048,1024]{1,0:T(8,128)(2,1)S(1)}, bf16[2048,1024]{1,0:T(8,128)(2,1)S(1)}, bf16[1024,1024]{1,0:T(8,128)(2,1)S(1)}, f32[4,1024]{1,0:T(4,128)S(1)}) custom-call(f32[128,1024]{1,0:T(8,128)} %new_hbm.1, f32[512,1024]{1,0:T(8,128)} %old_hbm.1, bf16[2048,1024]{1,0:T(8,128)(2,1)} %grm_hbm.1, s32[2]{0:T(128)} %counts_hbm.1, s32[2,4]{1,0:T(2,128)} %bitcast.1), custom_call_target="tpu_custom_call" | custom-call | tf_op jit(solution)/shard_map/pallas_call | solution.py:656
  28.9 2.0 %shard_map.56 = bf16[2048,1024]{1,0:T(8,128)(2,1)} custom-call(bf16[2048,1024]{1,0:T(8,128)(2,1)S(1)} %get-tuple-element.9.res, bf16[2048,1024]{1,0:T(8,128)(2,1)S(1)} %get-tuple-element.10.old_buf, bf16[1024,1024]{1,0:T(8,128)(2,1)S(1)} %get-tuple-element.11.new_buf, f32[4,1024]{1,0:T(4,128)S(1)} %get-tuple-element.12.gain), custom_call_target="tpu_custom_call" | custom-call | tf_op jit(solution)/shard_map/pallas_call | solution.py:690

commit v5 on v4

--- a/solution.py
+++ b/solution.py
@@ -45,7 +45,7 @@
     n_row, n_col, new_hbm, old_hbm, grm_hbm, counts_hbm, affected_hbm,
     res, old_buf, new_buf, gain,
     new_in, old_in, new_code, old_code, part, part_y, part_z, counts, affected,
-    load_sem, sum_recv, far, x_recv, sib_recv, own_recv, new_recv, sent,
+    load_sem, sum_recv, far, near, x_recv, sib_recv, own_recv, new_recv, sent,
 ):
     snps = new_in.shape[1]
     new_rows, old_rows = new_in.shape[0], old_in.shape[0]
@@ -92,8 +92,9 @@
     def greet(device):
         pl.semaphore_signal(barrier, inc=1, device_id=device, device_id_type=MESH)
 
-    for d in range(1, n_col):
-        greet((row, (col + d) % n_col))
+    greet((row, sibling))
+    for d in range(1, chips):
+        greet((row, (chip + d) % chips * CORES + core))
     for d in range(1, minor):
         greet((a * minor + (b + d) % minor, col))
 
@@ -270,11 +271,13 @@
     with jax.named_scope("barrier"):
         pl.semaphore_wait(
             barrier,
-            n_col - 1 + minor - 1 + has_left.astype(jnp.int32) + has_right.astype(jnp.int32),
+            chips + minor - 1 + has_left.astype(jnp.int32) + has_right.astype(jnp.int32),
         )
     send_old(0)
     send_z(0)
+    send_y(a, final, lender)
     far_tell(2)
+    pl.semaphore_signal(near.at[0], inc=1, device_id=(row, sibling), device_id_type=MESH)
     with jax.named_scope("loadold"):
         old_loads[1].wait()
         mine = jnp.sum(old_in[...], axis=0, keepdims=True)
@@ -282,7 +285,8 @@
             part_y[pl.ds(b, 1), f, :] = mine[:, f * FOLD:(f + 1) * FOLD]
         send_sums(*over_mid)
     with jax.named_scope("first"):
-        for k in range(NEW_CHUNKS):
+        send_y(a, final, taker)
+        for k in reversed(range(final)):
             send_y(a, k)
         for k in range(1, CODED):
             encode_old(k)
@@ -332,15 +336,16 @@
     def own_first():
         for d in range(1, minor):
             r = a * minor + (b + d) % minor
-            new_copy(r, final, row).wait_recv()
+
+            @pl.when(is_end(a))
+            def _():
+                new_copy(r, final, row).wait_recv()
             start(new_copy(r, final, row + minor), a == 0)
             start(new_copy(r, final, row - minor), a == major - 1)
 
-    def wait_y(t):
+    def wait_y(t, first=0, stop=NEW_CHUNKS):
         z = slot_place(a, major, t)
-        for k in range(NEW_CHUNKS):
-            if t == 0 and k == final:
-                continue
+        for k in range(first, stop):
             for d in range(1, minor):
                 r = z * minor + (b + d) % minor
                 copy = new_copy(r, k, row)
@@ -427,16 +432,17 @@
 
     with jax.named_scope("relay0"):
         relay(0, 0)
+    with jax.named_scope("own_first"):
+        own_first()
     with jax.named_scope("sumz"):
         part[col] = take_sums(*over_row)
+        pl.semaphore_wait(near.at[0], 1)
         send_sums(*over_col)
         for k in range(AHEAD, CODED):
             send_old(k)
     with jax.named_scope("relay1"):
         for k in range(1, NEW_CHUNKS):
             relay(0, k)
-    with jax.named_scope("own_first"):
-        own_first()
     with jax.named_scope("x0"):
         forward_old(0)
     with jax.named_scope("sumcol"):
@@ -466,17 +472,17 @@
     def decode(codes):
         return codes.astype(jnp.int32).astype(jnp.float32) * code_scale + code_shift
 
-    def decode_new(t):
+    def decode_new(t, lead=0, rows=None):
         z = slot_place(a, major, t)
         count = counts[(z * group) // tile]
 
-        @pl.loop(0, group // STRIP)
+        @pl.loop(0, (rows or group) // STRIP)
         def _(i):
-            at = z * group + i * STRIP
+            at = z * group + lead + i * STRIP
             place = lax.broadcasted_iota(jnp.int32, (STRIP, 1), 0) + at % tile
             usable = (place < count).astype(jnp.float32)
             codes = new_code[ds(at, STRIP, STRIP), :]
-            new_buf[ds(t * group + i * STRIP, STRIP, STRIP), :] = (
+            new_buf[ds(t * group + lead + i * STRIP, STRIP, STRIP), :] = (
                 decode(codes) * usable
             ).astype(jnp.bfloat16)
 
@@ -561,8 +567,16 @@
         local(t, 1)
         distant(0, LATE, t, 1)
     forwarded(3)
+    with jax.named_scope("early"):
+        decode_new(major - 1, b * new_rows, new_rows)
+        wait_y(major - 1, 0, final)
+        for d in range(1, minor):
+            decode_new(major - 1, (b + d) % minor * new_rows, final * new_chunk)
     relayed_first(major - 2)
-    take_group(major - 1)
+    with jax.named_scope("rest"):
+        wait_y(major - 1, final)
+        for d in range(1, minor):
+            decode_new(major - 1, (b + d) % minor * new_rows + final * new_chunk, new_chunk)
     local(major - 1, 1)
     forwarded(4)
     distant(0, LATE, major - 1, 1)
@@ -676,6 +690,7 @@
             dma((6,)),
             dma((3,)),
             pltpu.SemaphoreType.REGULAR((max(1, major - 2),)),
+            pltpu.SemaphoreType.REGULAR((1,)),
             dma((chips - 1, pieces + 1)),
             dma((chips - 1, pieces + 1)),
             dma((1,)),

time: 31.1 us -> 31 us (level)
  no operation moved by 1% of the time
where the time goes in v5:
time: 31 us; the launch traced here: 30.9 us
  Pallas kernels  30.9 us (100%)
    pallas_call x1, Pallas kernels, on_device(): pl.pallas_call(functools.partial(kernel, n_row, n_col), out_shape=(pltpu....  28.8 us
    pallas_call x1, Pallas kernels, on_device(): pl.pallas_call(functools.partial(finish, n_row, n_col), out_shape=jax.Sha...  2.03 us

profile of v5, /device:TPU:0, one launch (start us, length us, event | category | flops | bytes accessed | tf_op | source)
XLA Modules:
  0.0 30.9 jit_solution(4575080538391703738)
XLA Ops:
  0.0 28.8 %shard_map.55 = (bf16[2048,1024]{1,0:T(8,128)(2,1)S(1)}, bf16[2048,1024]{1,0:T(8,128)(2,1)S(1)}, bf16[1024,1024]{1,0:T(8,128)(2,1)S(1)}, f32[4,1024]{1,0:T(4,128)S(1)}) custom-call(f32[128,1024]{1,0:T(8,128)} %new_hbm.1, f32[512,1024]{1,0:T(8,128)} %old_hbm.1, bf16[2048,1024]{1,0:T(8,128)(2,1)} %grm_hbm.1, s32[2]{0:T(128)} %counts_hbm.1, s32[2,4]{1,0:T(2,128)} %bitcast.1), custom_call_target="tpu_custom_call" | custom-call | tf_op jit(solution)/shard_map/pallas_call | solution.py:670
  28.8 2.0 %shard_map.56 = bf16[2048,1024]{1,0:T(8,128)(2,1)} custom-call(bf16[2048,1024]{1,0:T(8,128)(2,1)S(1)} %get-tuple-element.9.res, bf16[2048,1024]{1,0:T(8,128)(2,1)S(1)} %get-tuple-element.10.old_buf, bf16[1024,1024]{1,0:T(8,128)(2,1)S(1)} %get-tuple-element.11.new_buf, f32[4,1024]{1,0:T(4,128)S(1)} %get-tuple-element.12.gain), custom_call_target="tpu_custom_call" | custom-call | tf_op jit(solution)/shard_map/pallas_call | solution.py:705

commit v6 on v5

--- a/solution.py
+++ b/solution.py
@@ -45,7 +45,7 @@
     n_row, n_col, new_hbm, old_hbm, grm_hbm, counts_hbm, affected_hbm,
     res, old_buf, new_buf, gain,
     new_in, old_in, new_code, old_code, part, part_y, part_z, counts, affected,
-    load_sem, sum_recv, far, near, x_recv, sib_recv, own_recv, new_recv, sent,
+    load_sem, sum_recv, far, x_recv, sib_recv, own_recv, new_recv, sent,
 ):
     snps = new_in.shape[1]
     new_rows, old_rows = new_in.shape[0], old_in.shape[0]
@@ -92,9 +92,8 @@
     def greet(device):
         pl.semaphore_signal(barrier, inc=1, device_id=device, device_id_type=MESH)
 
-    greet((row, sibling))
-    for d in range(1, chips):
-        greet((row, (chip + d) % chips * CORES + core))
+    for d in range(1, n_col):
+        greet((row, (col + d) % n_col))
     for d in range(1, minor):
         greet((a * minor + (b + d) % minor, col))
 
@@ -271,13 +270,11 @@
     with jax.named_scope("barrier"):
         pl.semaphore_wait(
             barrier,
-            chips + minor - 1 + has_left.astype(jnp.int32) + has_right.astype(jnp.int32),
+            n_col - 1 + minor - 1 + has_left.astype(jnp.int32) + has_right.astype(jnp.int32),
         )
     send_old(0)
     send_z(0)
-    send_y(a, final, lender)
     far_tell(2)
-    pl.semaphore_signal(near.at[0], inc=1, device_id=(row, sibling), device_id_type=MESH)
     with jax.named_scope("loadold"):
         old_loads[1].wait()
         mine = jnp.sum(old_in[...], axis=0, keepdims=True)
@@ -285,8 +282,7 @@
             part_y[pl.ds(b, 1), f, :] = mine[:, f * FOLD:(f + 1) * FOLD]
         send_sums(*over_mid)
     with jax.named_scope("first"):
-        send_y(a, final, taker)
-        for k in reversed(range(final)):
+        for k in reversed(range(NEW_CHUNKS)):
             send_y(a, k)
         for k in range(1, CODED):
             encode_old(k)
@@ -436,7 +432,6 @@
         own_first()
     with jax.named_scope("sumz"):
         part[col] = take_sums(*over_row)
-        pl.semaphore_wait(near.at[0], 1)
         send_sums(*over_col)
         for k in range(AHEAD, CODED):
             send_old(k)
@@ -690,7 +685,6 @@
             dma((6,)),
             dma((3,)),
             pltpu.SemaphoreType.REGULAR((max(1, major - 2),)),
-            pltpu.SemaphoreType.REGULAR((1,)),
             dma((chips - 1, pieces + 1)),
             dma((chips - 1, pieces + 1)),
             dma((1,)),

time: 31 us -> 31 us (level)
  no operation moved by 1% of the time
where the time goes in v6:
time: 31 us; the launch traced here: 30.9 us
  Pallas kernels  30.9 us (100%)
    pallas_call x1, Pallas kernels, on_device(): pl.pallas_call(functools.partial(kernel, n_row, n_col), out_shape=(pltpu....  28.8 us
    pallas_call x1, Pallas kernels, on_device(): pl.pallas_call(functools.partial(finish, n_row, n_col), out_shape=jax.Sha...  2.03 us

profile of v6, /device:TPU:0, one launch (start us, length us, event | category | flops | bytes accessed | tf_op | source)
XLA Modules:
  0.0 30.9 jit_solution(9353975269325956543)
XLA Ops:
  0.0 28.8 %shard_map.55 = (bf16[2048,1024]{1,0:T(8,128)(2,1)S(1)}, bf16[2048,1024]{1,0:T(8,128)(2,1)S(1)}, bf16[1024,1024]{1,0:T(8,128)(2,1)S(1)}, f32[4,1024]{1,0:T(4,128)S(1)}) custom-call(f32[128,1024]{1,0:T(8,128)} %new_hbm.1, f32[512,1024]{1,0:T(8,128)} %old_hbm.1, bf16[2048,1024]{1,0:T(8,128)(2,1)} %grm_hbm.1, s32[2]{0:T(128)} %counts_hbm.1, s32[2,4]{1,0:T(2,128)} %bitcast.1), custom_call_target="tpu_custom_call" | custom-call | tf_op jit(solution)/shard_map/pallas_call | solution.py:665
  28.8 2.0 %shard_map.56 = bf16[2048,1024]{1,0:T(8,128)(2,1)} custom-call(bf16[2048,1024]{1,0:T(8,128)(2,1)S(1)} %get-tuple-element.9.res, bf16[2048,1024]{1,0:T(8,128)(2,1)S(1)} %get-tuple-element.10.old_buf, bf16[1024,1024]{1,0:T(8,128)(2,1)S(1)} %get-tuple-element.11.new_buf, f32[4,1024]{1,0:T(4,128)S(1)} %get-tuple-element.12.gain), custom_call_target="tpu_custom_call" | custom-call | tf_op jit(solution)/shard_map/pallas_call | solution.py:699
